TPU v7x, 32 devices: a whole 2x2x4 slice. The times are simulated.
32 devices in a mesh: img: 2 (over x), ga: 4 (over y, core), band: 4 (over z).
Axes of the slice: x: 2, y: 2, z: 4, core: 2. Of those that a mesh axis runs over, the one named last changes fastest.
Arguments:
- orbitals: bfloat16 [1536, 12288], P(('img', 'band'), 'ga'), parts along dimension 0, as said below
- kernel: float32 [12288], P('ga'), may hold values from 0.3 to 3
- block_vectors: bfloat16 [512, 12288], P(('img', 'band'), 'ga'), parts along dimension 0
Outputs:
- ace_vectors: bfloat16 [1536, 12288], P(('img', 'band'), 'ga'), parts along dimension 0
- exchange_block: bfloat16 [512, 12288], P(('img', 'band'), 'ga'), parts along dimension 0
There are 2 independent parts, one for each index of `img`. A program takes and returns all parts, laid end to end along the dimension named above; an argument that names none is the same for every part. Nothing has to cross between parts.
Inputs may be any that keep to these rules, and one draw needn't show every extreme that they name: `orbitals`: the bands of one image are linearly independent, and the block lies largely in their span.
All inputs are finite; a program needn't handle non-finite values.
Results may differ from a plain program's by a relative error of at most 0.02.
Values may be sent and summed in bfloat16 or wider, within the bound.
A program may use at most 64 MiB of HBM per device.

v0:
```python
import jax
import jax.numpy as jnp
from jax import lax
from jax.sharding import PartitionSpec as P


def contract_first(left, right):
    return lax.dot_general(left, right, (((0,), (0,)), ((), ())), precision=lax.Precision.HIGHEST)


def shards(orbitals, kernel, block_vectors):
    groups = lax.axis_size("ga")
    own_band = lax.axis_index("band")
    total_coeffs = orbitals.shape[1] * groups
    full_orbitals, full_block = (
        lax.all_gather(orbitals, "band", axis=0, tiled=True),
        lax.all_gather(block_vectors, "band", axis=0, tiled=True),
    )
    weighted = (-(full_orbitals.astype(jnp.float32) * kernel[None, :])).astype(jnp.bfloat16)
    own_rows = orbitals.shape[0]
    partial_rows = lax.dot_general(
        orbitals, weighted, (((1,), (1,)), ((), ())), preferred_element_type=jnp.float32
    )
    summed_rows = lax.psum(partial_rows.astype(jnp.bfloat16), "ga").astype(jnp.float32)
    margin = -lax.all_gather(summed_rows, "band", axis=0, tiled=True) / total_coeffs
    factor = jnp.linalg.cholesky(margin)
    identity = jnp.eye(factor.shape[0], dtype=jnp.float32)
    inverse = lax.linalg.triangular_solve(factor, identity, left_side=True, lower=True)
    inverse_rows = lax.dynamic_slice_in_dim(inverse, own_band * own_rows, own_rows, 0)
    projector = jnp.dot(inverse_rows, weighted.astype(jnp.float32), precision=lax.Precision.HIGHEST)
    local_coupling = jnp.dot(
        projector, full_block.astype(jnp.float32).T, precision=lax.Precision.HIGHEST
    )
    coupling = (
        lax.psum(local_coupling.astype(jnp.bfloat16), "ga").astype(jnp.float32) / total_coeffs
    )
    applied = lax.psum_scatter(
        -contract_first(coupling, projector), "band", scatter_dimension=0, tiled=True
    )
    return (projector.astype(jnp.bfloat16), applied.astype(jnp.bfloat16))


def solution(mesh):
    placed = (P(("img", "band"), "ga"), P("ga"), P(("img", "band"), "ga"))
    return jax.shard_map(
        shards,
        mesh=mesh,
        in_specs=placed,
        out_specs=(P(("img", "band"), "ga"), P(("img", "band"), "ga")),
        check_vma=False,
    )
```

profile of v0, /device:TPU:0, one launch (start us, length us, event | category | flops | bytes accessed | tf_op | source)
XLA Modules:
  0.0 548.5 jit_solution(6717364289099904385)
XLA Ops:
  7.2 0.7 all-gather.4.cloned.1.call-update
  7.9 93.7 %all-gather.4.cloned.1.call-done = bf16[768,3072]{1,0:T(8,128)(2,1)} async-done(((bf16[192,3072]{1,0:T(8,128)(2,1)}), bf16[768,3072]{1,0:T(8,128)(2,1)}) %all-gather.4.cloned.1.call-update) | async-done | bytes 4718608 | tf_op jit(solution)/shard_map/all_gather | solution.py:16
  101.7 5.1 fusion.20
  106.9 30.9 %all-reduce.4.cloned.1.call-done = bf16[192,768]{1,0:T(8,128)(2,1)} async-done(((bf16[192,768]{1,0:T(8,128)(2,1)}), bf16[192,768]{1,0:T(8,128)(2,1)}) %all-reduce.4.cloned.1.call-update) | async-done | bytes 294928 | tf_op jit(solution)/shard_map/psum | solution.py:24
  137.8 1.8 convert_element_type.44
  140.5 1.6 fusion.24
  142.1 47.9 %all-gather.6.cloned.1.call-done = f32[768,768]{1,0:T(8,128)} async-done(((f32[192,768]{1,0:T(8,128)}), f32[768,768]{1,0:T(8,128)}) %all-gather.6.cloned.1.call-update) | async-done | bytes 2359312 | tf_op jit(solution)/shard_map/all_gather | solution.py:25
  190.0 2.0 copy.7
  192.1 1.7 negate_multiply_fusion
  193.7 3.2 copy.8
  197.0 2.1 fusion.2
  199.0 1.5 copy-done.1
  200.5 11.7 %cholesky.165 = f32[128,128]{1,0:T(8,128)S(1)} custom-call(f32[128,128]{1,0:T(8,128)S(1)} %cholesky.424), custom_call_target="Cholesky" | custom-call | tf_op jit(solution)/shard_map/jit(cholesky)/cholesky | solution.py:26
  212.3 9.8 %custom-call.46 = f32[1,128,128]{1,2,0:T(8,128)S(1)} custom-call(f32[1,128,128]{2,1,0:T(8,128)S(1)} %get-tuple-element.45), custom_call_target="InvertDiagBlocksLowerTriangular" | custom-call | tf_op jit(solution)/shard_map/jit(cholesky)/cholesky | solution.py:26
  222.2 1.4 constant_dynamic-update-slice_fusion.15
  223.6 1.4 convolution_subtract_fusion.4
  225.0 11.7 %cholesky.188 = f32[128,128]{1,0:T(8,128)S(1)} custom-call(f32[128,128]{1,0:T(8,128)S(1)} %cholesky.428), custom_call_target="Cholesky" | custom-call | tf_op jit(solution)/shard_map/jit(cholesky)/cholesky | solution.py:26
  236.8 10.0 %custom-call.47 = f32[1,128,128]{1,2,0:T(8,128)S(1)} custom-call(f32[1,128,128]{2,1,0:T(8,128)S(1)} %get-tuple-element.42), custom_call_target="InvertDiagBlocksLowerTriangular" | custom-call | tf_op jit(solution)/shard_map/jit(cholesky)/cholesky | solution.py:26
  247.2 1.5 convolution_subtract_fusion.5
  248.7 11.7 %cholesky.354 = f32[128,128]{1,0:T(8,128)S(1)} custom-call(f32[128,128]{1,0:T(8,128)S(1)} %cholesky.433), custom_call_target="Cholesky" | custom-call | tf_op jit(solution)/shard_map/jit(cholesky)/cholesky | solution.py:26
  260.5 0.7 compare_reduce_fusion.3
  261.2 9.8 %custom-call.48 = f32[1,128,128]{1,2,0:T(8,128)S(1)} custom-call(f32[1,128,128]{2,1,0:T(8,128)S(1)} %get-tuple-element.39), custom_call_target="InvertDiagBlocksLowerTriangular" | custom-call | tf_op jit(solution)/shard_map/jit(cholesky)/cholesky | solution.py:26
  271.3 1.6 convolution_subtract_fusion.6
  272.9 12.2 %cholesky.373 = f32[128,128]{1,0:T(8,128)S(1)} custom-call(f32[128,128]{1,0:T(8,128)S(1)} %cholesky.438), custom_call_target="Cholesky" | custom-call | tf_op jit(solution)/shard_map/jit(cholesky)/cholesky | solution.py:26
  285.1 0.7 compare_reduce_fusion.2
  285.8 9.8 %custom-call.49 = f32[1,128,128]{1,2,0:T(8,128)S(1)} custom-call(f32[1,128,128]{2,1,0:T(8,128)S(1)} %get-tuple-element.36), custom_call_target="InvertDiagBlocksLowerTriangular" | custom-call | tf_op jit(solution)/shard_map/jit(cholesky)/cholesky | solution.py:26
  295.9 1.5 convolution_subtract_fusion.7
  297.4 11.7 %cholesky.392 = f32[128,128]{1,0:T(8,128)S(1)} custom-call(f32[128,128]{1,0:T(8,128)S(1)} %cholesky.443), custom_call_target="Cholesky" | custom-call | tf_op jit(solution)/shard_map/jit(cholesky)/cholesky | solution.py:26
  309.1 0.7 compare_reduce_fusion.1
  309.8 9.8 %custom-call.50 = f32[1,128,128]{1,2,0:T(8,128)S(1)} custom-call(f32[1,128,128]{2,1,0:T(8,128)S(1)} %get-tuple-element.33), custom_call_target="InvertDiagBlocksLowerTriangular" | custom-call | tf_op jit(solution)/shard_map/jit(cholesky)/cholesky | solution.py:26
  319.9 1.3 convolution_subtract_fusion.8
  321.2 11.9 %cholesky.410 = f32[128,128]{1,0:T(8,128)S(1)} custom-call(f32[128,128]{1,0:T(8,128)S(1)} %convolution_subtract_fusion.8), custom_call_target="Cholesky" | custom-call | tf_op jit(solution)/shard_map/jit(cholesky)/cholesky | solution.py:26
  333.1 0.7 compare_reduce_fusion
  333.8 0.7 compare_reduce_fusion.4
  338.4 1.6 select_select_fusion
  340.0 21.3 %while.1 = (s32[]{:T(128)}, f32[768,768]{1,0:T(8,128)}, s32[6,2]{0,1:T(2,128)S(1)}, f32[6,128,128]{2,1,0:T(8,128)}, s32[]{:T(128)}) while((s32[]{:T(128)}, f32[768,768]{1,0:T(8,128)}, s32[6,2]{0,1:T(2,128)S(1)}, f32[6,128,128]{2,1,0:T(8,128)}, s32[]{:T(128)}) %tuple.45), condition=%wide.while_cond, body=%wide.while_body.sunk | while | flops 2 | bytes 132705 | solution.py:28
  340.1 0.6 fusion.79
  340.6 3.0 bitcast_dynamic-update-slice_fusion.2
  343.7 0.6 fusion.79
  344.3 2.9 bitcast_dynamic-update-slice_fusion.2
  347.2 0.6 fusion.79
  347.8 2.9 bitcast_dynamic-update-slice_fusion.2
  350.8 0.6 fusion.79
  351.4 2.9 bitcast_dynamic-update-slice_fusion.2
  354.3 0.6 fusion.79
  354.9 2.9 bitcast_dynamic-update-slice_fusion.2
  357.9 0.6 fusion.79
  358.4 2.8 bitcast_dynamic-update-slice_fusion.2
  361.3 60.4 %custom-call.51 = f32[6,128,128]{1,2,0:T(8,128)} custom-call(f32[6,128,128]{2,1,0:T(8,128)} %get-tuple-element.9), custom_call_target="InvertDiagBlocksLowerTriangular" | custom-call | tf_op jit(solution)/shard_map/triangular_solve | solution.py:28
  421.7 1.3 constant_dynamic-update-slice_fusion.4
  423.0 1.5 convolution_subtract_fusion.2
  424.5 0.5 constant_dynamic-update-slice_fusion.3
  425.1 1.5 convolution_subtract_fusion.3
  426.5 0.5 constant_dynamic-update-slice_fusion.2
  427.1 2.0 convolution_subtract_fusion.1
  429.1 0.5 constant_dynamic-update-slice_fusion.1
  429.6 2.0 fusion.12
  432.2 2.3 convolution_subtract_fusion
  435.0 4.2 fusion.65
  439.3 3.8 convolution_convert_fusion
  443.4 30.3 %all-reduce.6.cloned.1.call-done = bf16[192,256]{1,0:T(8,128)(2,1)} async-done(((bf16[192,256]{1,0:T(8,128)(2,1)}), bf16[192,256]{1,0:T(8,128)(2,1)}) %all-reduce.6.cloned.1.call-update) | async-done | bytes 98320 | tf_op jit(solution)/shard_map/psum | solution.py:35
  473.6 5.3 convolution_negate_fusion
  479.0 60.6 %reduce-scatter.2.cloned.1.call-done = f32[64,3072]{1,0:T(8,128)} async-done(((f32[256,3072]{1,0:T(8,128)}), f32[64,3072]{1,0:T(8,128)}) %reduce-scatter.2.cloned.1.call-update) | async-done | bytes 786448 | tf_op jit(solution)/shard_map/reduce_scatter | solution.py:37
  539.5 1.9 convert_element_type.49
  (52 shorter events, 4.3 us)
Async XLA Ops:
  7.2 94.5 %all-gather.4.cloned.1.call-start = ((), (), s32[]{:S(2)}) async-start(), calls=%async_computation.1 | async-start | bytes 5898240 | tf_op jit(solution)/shard_map/all_gather | solution.py:16
  7.9 130.0 %all-reduce.4.cloned.1.call-start = ((), (), s32[]{:S(2)}) async-start(), calls=%async_computation.2 | async-start | bytes 589824 | tf_op jit(solution)/shard_map/psum | solution.py:24
  106.9 83.2 %all-gather.6.cloned.1.call-start = ((), (), s32[]{:S(2)}) async-start(), calls=%async_computation.3 | async-start | bytes 2949120 | tf_op jit(solution)/shard_map/all_gather | solution.py:25
  139.7 299.6 %all-gather.8.cloned.1.call-start = ((), (), s32[]{:S(2)}) async-start(), calls=%async_computation.4 | async-start | bytes 1966080 | tf_op jit(solution)/shard_map/all_gather | solution.py:17
  140.3 333.4 %all-reduce.6.cloned.1.call-start = ((), (), s32[]{:S(2)}) async-start(), calls=%async_computation.5 | async-start | bytes 196608 | tf_op jit(solution)/shard_map/psum | solution.py:35
  199.0 1.5 copy-start.1
  340.0 85.0 %copy-start = (f32[768,768]{1,0:T(8,128)S(1)}, f32[768,768]{1,0:T(8,128)}, u32[]{:S(2)}) copy-start(f32[768,768]{1,0:T(8,128)} %fusion.24) | copy-start | bytes 7077892
  421.7 2.8 copy-start.2
  427.1 7.9 %slice-start = ((s8[4718592]{0:T(1024)(128)(4,1)}), s8[4194304]{0:T(1024)(128)(4,1)S(1)}, s32[]{:S(2)}) async-start(s8[4718592]{0:T(1024)(128)(4,1)} %bitcast.83), calls=%async_computation.7 | async-start | bytes 8388608
  429.6 5.4 slice-start.1
  431.6 3.4 copy-start.3
  443.1 96.4 %reduce-scatter.2.cloned.1.call-start = ((), (), s32[]{:S(2)}) async-start(), calls=%async_computation.6 | async-start | bytes 3932160 | tf_op jit(solution)/shard_map/reduce_scatter | solution.py:37
Sparse Core Ops, SparseCore 0:
  9.5 92.1 all-gather.3
  107.0 30.8 all-reduce.3
  140.0 49.9 all-gather.5
  191.4 35.7 all-gather.7
  443.2 30.3 all-reduce.5
  479.1 60.3 reduce-scatter.1
where the time goes:
time: 552 us; the launch traced here: 549 us
  waiting for transfers between devices  265 us (48%)
  other arithmetic  195 us (35%)
  matrix products  41.5 us (8%)
  local copies, waits for them, and re-layouts  28.2 us (5%)
  between operations  18.6 us (3%)
    another operation x22, other arithmetic, shards(): factor = jnp.linalg.cholesky(margin)  124 us
    all_gather x1, waiting for transfers between devices, shards(): lax.all_gather(orbitals, 'band', axis=0, tiled=True)  93.7 us
    another operation x3, other arithmetic, shards(): lax.linalg.triangular_solve(factor, identity, left_side=True, lower=True)  62 us
    reduce_scatter x1, waiting for transfers between devices, shards(): lax.psum_scatter(-contract_first(coupling, projector), 'band', scatter_di...  60.6 us
    all_gather x1, waiting for transfers between devices, shards(): lax.all_gather(summed_rows, 'band', axis=0, tiled=True)  47.9 us
    psum x1, waiting for transfers between devices, shards(): lax.psum(partial_rows.astype(jnp.bfloat16), 'ga').astype(jnp.float32)  30.9 us
    psum x1, waiting for transfers between devices, shards(): lax.psum(local_coupling.astype(jnp.bfloat16), 'ga').astype(jnp.float32)  30.3 us
    another operation x18, local copies, waits for them, and re-layouts  21.3 us
  transfers between devices with their start and end apart: 6, of which 5 were waited for; matrix products, arithmetic and copies ran while one was open for 45% of the time, Pallas kernels for 0%

commit v1 on v0

--- a/solution.py
+++ b/solution.py
@@ -1,7 +1,18 @@
+import functools
 import jax
 import jax.numpy as jnp
 from jax import lax
 from jax.sharding import PartitionSpec as P
+
+
+def compute_region_for(page, array_axis):
+    main = lax.all_to_all(
+        jnp.stack(tuple((page for _ in range(lax.axis_size("band")))), axis=0), "band", 0, 0
+    )
+    return jnp.concatenate(main, axis=array_axis)
+
+
+leaf_rest = functools.partial(compute_region_for, array_axis=0)
 
 
 def contract_first(left, right):
@@ -22,7 +33,7 @@
         orbitals, weighted, (((1,), (1,)), ((), ())), preferred_element_type=jnp.float32
     )
     summed_rows = lax.psum(partial_rows.astype(jnp.bfloat16), "ga").astype(jnp.float32)
-    margin = -lax.all_gather(summed_rows, "band", axis=0, tiled=True) / total_coeffs
+    margin = -leaf_rest(summed_rows) / total_coeffs
     factor = jnp.linalg.cholesky(margin)
     identity = jnp.eye(factor.shape[0], dtype=jnp.float32)
     inverse = lax.linalg.triangular_solve(factor, identity, left_side=True, lower=True)

time: 552 us -> 582 us (1.054)
  waiting for transfers between devices: 265 us -> 293 us
    all_to_all x0 -> x1, waiting for transfers between devices: none -> 75.5 us  [compute_region_for(): lax.all_to_all(jnp.stack(tuple((page for _ in range(lax.axis_size('band')...]
    all_gather x1 -> x0, waiting for transfers between devices: 47.9 us -> none  [shards(): lax.all_gather(summed_rows, 'band', axis=0, tiled=True)]
    another operation x18 -> x19, local copies, waits for them, and re-layouts: 21.3 us -> 24.1 us
  transfers between devices with their start and end apart: 6 -> 6, of which waited for: 5 -> 5; matrix products, arithmetic and copies ran while one was open for 45% -> 42% of each run, Pallas kernels for 0% -> 0%
where the time goes in v1:
time: 582 us; the launch traced here: 579 us
  waiting for transfers between devices  293 us (50%)
  other arithmetic  193 us (33%)
  matrix products  41.5 us (7%)
  local copies, waits for them, and re-layouts  28 us (5%)
  between operations  18.2 us (3%)
    another operation x22, other arithmetic, shards(): factor = jnp.linalg.cholesky(margin)  124 us
    all_gather x1, waiting for transfers between devices, shards(): lax.all_gather(orbitals, 'band', axis=0, tiled=True)  93.7 us
    all_to_all x1, waiting for transfers between devices, compute_region_for(): lax.all_to_all(jnp.stack(tuple((page for _ in range(lax.axis_size('band')...  75.5 us
    another operation x3, other arithmetic, shards(): lax.linalg.triangular_solve(factor, identity, left_side=True, lower=True)  62 us
    reduce_scatter x1, waiting for transfers between devices, shards(): lax.psum_scatter(-contract_first(coupling, projector), 'band', scatter_di...  60.6 us
    psum x1, waiting for transfers between devices, shards(): lax.psum(partial_rows.astype(jnp.bfloat16), 'ga').astype(jnp.float32)  31 us
    psum x1, waiting for transfers between devices, shards(): lax.psum(local_coupling.astype(jnp.bfloat16), 'ga').astype(jnp.float32)  30.3 us
    another operation x18, local copies, waits for them, and re-layouts  21.5 us
  transfers between devices with their start and end apart: 6, of which 5 were waited for; matrix products, arithmetic and copies ran while one was open for 42% of the time, Pallas kernels for 0%

profile of v1, /device:TPU:0, one launch (start us, length us, event | category | flops | bytes accessed | tf_op | source)
XLA Modules:
  0.0 578.5 jit_solution(12851269268081294261)
XLA Ops:
  7.2 0.7 all-gather.3.cloned.1.call-update
  7.9 93.7 %all-gather.3.cloned.1.call-done = bf16[768,3072]{1,0:T(8,128)(2,1)} async-done(((bf16[192,3072]{1,0:T(8,128)(2,1)}), bf16[768,3072]{1,0:T(8,128)(2,1)}) %all-gather.3.cloned.1.call-update) | async-done | bytes 4718608 | tf_op jit(solution)/shard_map/all_gather | solution.py:27
  101.7 5.1 fusion.20
  106.9 31.0 %all-reduce.4.cloned.1.call-done = bf16[192,768]{1,0:T(8,128)(2,1)} async-done(((bf16[192,768]{1,0:T(8,128)(2,1)}), bf16[192,768]{1,0:T(8,128)(2,1)}) %all-reduce.4.cloned.1.call-update) | async-done | bytes 294928 | tf_op jit(solution)/shard_map/psum | solution.py:35
  137.8 2.6 stack.2
  140.4 4.6 all-to-all-start
  145.0 0.7 all-gather.5.cloned.1.call-update
  146.0 1.6 fusion.24
  147.6 75.5 %all-to-all-done = f32[4,192,768]{2,1,0:T(8,128)} async-done(((f32[4,192,768]{2,1,0:T(8,128)}), f32[4,192,768]{2,1,0:T(8,128)}, u32[]{:S(2)}, u32[]{:S(2)}) %all-to-all-start) | async-done | bytes 2359328 | tf_op jit(solution)/shard_map/all_to_all | solution.py:9
  223.2 1.9 negate_multiply_fusion
  225.0 2.2 copy.7
  227.2 1.9 fusion.2
  229.1 1.5 copy-done.1
  230.6 11.7 %cholesky.165 = f32[128,128]{1,0:T(8,128)S(1)} custom-call(f32[128,128]{1,0:T(8,128)S(1)} %cholesky.424), custom_call_target="Cholesky" | custom-call | tf_op jit(solution)/shard_map/jit(cholesky)/cholesky | solution.py:37
  242.3 9.8 %custom-call.46 = f32[1,128,128]{1,2,0:T(8,128)S(1)} custom-call(f32[1,128,128]{2,1,0:T(8,128)S(1)} %get-tuple-element.45), custom_call_target="InvertDiagBlocksLowerTriangular" | custom-call | tf_op jit(solution)/shard_map/jit(cholesky)/cholesky | solution.py:37
  252.3 1.4 constant_dynamic-update-slice_fusion.15
  253.7 1.4 convolution_subtract_fusion.4
  255.1 11.7 %cholesky.188 = f32[128,128]{1,0:T(8,128)S(1)} custom-call(f32[128,128]{1,0:T(8,128)S(1)} %cholesky.428), custom_call_target="Cholesky" | custom-call | tf_op jit(solution)/shard_map/jit(cholesky)/cholesky | solution.py:37
  266.9 10.0 %custom-call.47 = f32[1,128,128]{1,2,0:T(8,128)S(1)} custom-call(f32[1,128,128]{2,1,0:T(8,128)S(1)} %get-tuple-element.42), custom_call_target="InvertDiagBlocksLowerTriangular" | custom-call | tf_op jit(solution)/shard_map/jit(cholesky)/cholesky | solution.py:37
  277.3 1.5 convolution_subtract_fusion.5
  278.8 11.7 %cholesky.354 = f32[128,128]{1,0:T(8,128)S(1)} custom-call(f32[128,128]{1,0:T(8,128)S(1)} %cholesky.433), custom_call_target="Cholesky" | custom-call | tf_op jit(solution)/shard_map/jit(cholesky)/cholesky | solution.py:37
  290.6 0.7 compare_reduce_fusion.3
  291.3 9.8 %custom-call.48 = f32[1,128,128]{1,2,0:T(8,128)S(1)} custom-call(f32[1,128,128]{2,1,0:T(8,128)S(1)} %get-tuple-element.39), custom_call_target="InvertDiagBlocksLowerTriangular" | custom-call | tf_op jit(solution)/shard_map/jit(cholesky)/cholesky | solution.py:37
  301.4 1.6 convolution_subtract_fusion.6
  303.0 12.2 %cholesky.373 = f32[128,128]{1,0:T(8,128)S(1)} custom-call(f32[128,128]{1,0:T(8,128)S(1)} %cholesky.438), custom_call_target="Cholesky" | custom-call | tf_op jit(solution)/shard_map/jit(cholesky)/cholesky | solution.py:37
  315.2 0.7 compare_reduce_fusion.2
  315.9 9.8 %custom-call.49 = f32[1,128,128]{1,2,0:T(8,128)S(1)} custom-call(f32[1,128,128]{2,1,0:T(8,128)S(1)} %get-tuple-element.36), custom_call_target="InvertDiagBlocksLowerTriangular" | custom-call | tf_op jit(solution)/shard_map/jit(cholesky)/cholesky | solution.py:37
  325.9 1.5 convolution_subtract_fusion.7
  327.5 11.7 %cholesky.392 = f32[128,128]{1,0:T(8,128)S(1)} custom-call(f32[128,128]{1,0:T(8,128)S(1)} %cholesky.443), custom_call_target="Cholesky" | custom-call | tf_op jit(solution)/shard_map/jit(cholesky)/cholesky | solution.py:37
  339.2 0.7 compare_reduce_fusion.1
  339.9 9.8 %custom-call.50 = f32[1,128,128]{1,2,0:T(8,128)S(1)} custom-call(f32[1,128,128]{2,1,0:T(8,128)S(1)} %get-tuple-element.33), custom_call_target="InvertDiagBlocksLowerTriangular" | custom-call | tf_op jit(solution)/shard_map/jit(cholesky)/cholesky | solution.py:37
  349.9 1.3 convolution_subtract_fusion.8
  351.3 11.9 %cholesky.410 = f32[128,128]{1,0:T(8,128)S(1)} custom-call(f32[128,128]{1,0:T(8,128)S(1)} %convolution_subtract_fusion.8), custom_call_target="Cholesky" | custom-call | tf_op jit(solution)/shard_map/jit(cholesky)/cholesky | solution.py:37
  363.2 0.7 compare_reduce_fusion
  363.9 0.7 compare_reduce_fusion.4
  368.4 1.6 select_select_fusion
  370.1 21.5 %while.1 = (s32[]{:T(128)}, f32[768,768]{1,0:T(8,128)}, s32[6,2]{0,1:T(2,128)S(1)}, f32[6,128,128]{2,1,0:T(8,128)}, s32[]{:T(128)}) while((s32[]{:T(128)}, f32[768,768]{1,0:T(8,128)}, s32[6,2]{0,1:T(2,128)S(1)}, f32[6,128,128]{2,1,0:T(8,128)}, s32[]{:T(128)}) %tuple.45), condition=%wide.while_cond, body=%wide.while_body.sunk | while | flops 2 | bytes 132705 | solution.py:39
  370.1 0.6 fusion.79
  370.7 3.0 bitcast_dynamic-update-slice_fusion.2
  373.8 0.6 fusion.79
  374.4 2.9 bitcast_dynamic-update-slice_fusion.2
  377.4 0.6 fusion.79
  378.0 2.9 bitcast_dynamic-update-slice_fusion.2
  381.0 0.6 fusion.79
  381.6 2.9 bitcast_dynamic-update-slice_fusion.2
  384.6 0.6 fusion.79
  385.1 2.9 bitcast_dynamic-update-slice_fusion.2
  388.2 0.6 fusion.79
  388.7 2.9 bitcast_dynamic-update-slice_fusion.2
  391.6 60.4 %custom-call.51 = f32[6,128,128]{1,2,0:T(8,128)} custom-call(f32[6,128,128]{2,1,0:T(8,128)} %get-tuple-element.9), custom_call_target="InvertDiagBlocksLowerTriangular" | custom-call | tf_op jit(solution)/shard_map/triangular_solve | solution.py:39
  452.0 1.3 constant_dynamic-update-slice_fusion.4
  453.3 1.5 convolution_subtract_fusion.2
  455.4 1.5 convolution_subtract_fusion.3
  456.9 0.5 constant_dynamic-update-slice_fusion.2
  457.4 2.0 convolution_subtract_fusion.1
  459.4 0.5 constant_dynamic-update-slice_fusion.1
  459.9 2.0 fusion.12
  462.5 2.3 convolution_subtract_fusion
  465.3 4.2 fusion.65
  469.6 3.8 convolution_convert_fusion
  473.7 30.3 %all-reduce.6.cloned.1.call-done = bf16[192,256]{1,0:T(8,128)(2,1)} async-done(((bf16[192,256]{1,0:T(8,128)(2,1)}), bf16[192,256]{1,0:T(8,128)(2,1)}) %all-reduce.6.cloned.1.call-update) | async-done | bytes 98320 | tf_op jit(solution)/shard_map/psum | solution.py:46
  504.0 5.3 convolution_negate_fusion
  509.3 60.6 %reduce-scatter.2.cloned.1.call-done = f32[64,3072]{1,0:T(8,128)} async-done(((f32[256,3072]{1,0:T(8,128)}), f32[64,3072]{1,0:T(8,128)}) %reduce-scatter.2.cloned.1.call-update) | async-done | bytes 786448 | tf_op jit(solution)/shard_map/reduce_scatter | solution.py:48
  569.8 1.9 convert_element_type.49
  (50 shorter events, 4.2 us)
Async XLA Ops:
  7.2 94.5 %all-gather.3.cloned.1.call-start = ((), (), s32[]{:S(2)}) async-start(), calls=%async_computation.2 | async-start | bytes 5898240 | tf_op jit(solution)/shard_map/all_gather | solution.py:27
  7.9 130.0 %all-reduce.4.cloned.1.call-start = ((), (), s32[]{:S(2)}) async-start(), calls=%async_computation.3 | async-start | bytes 589824 | tf_op jit(solution)/shard_map/psum | solution.py:35
  140.4 82.7 %all-to-all-start = ((f32[4,192,768]{2,1,0:T(8,128)}), f32[4,192,768]{2,1,0:T(8,128)}, u32[]{:S(2)}, u32[]{:S(2)}) async-start(f32[4,192,768]{2,1,0:T(8,128)} %stack.2), calls=%async_computation | async-start | bytes 4718592 | tf_op jit(solution)/shard_map/all_to_all | solution.py:9
  145.0 324.6 %all-gather.5.cloned.1.call-start = ((), (), s32[]{:S(2)}) async-start(), calls=%async_computation.4 | async-start | bytes 1966080 | tf_op jit(solution)/shard_map/all_gather | solution.py:28
  145.8 358.2 %all-reduce.6.cloned.1.call-start = ((), (), s32[]{:S(2)}) async-start(), calls=%async_computation.5 | async-start | bytes 196608 | tf_op jit(solution)/shard_map/psum | solution.py:46
  229.1 1.5 copy-start.1
  370.1 85.3 %copy-start = (f32[768,768]{1,0:T(8,128)S(1)}, f32[768,768]{1,0:T(8,128)}, u32[]{:S(2)}) copy-start(f32[768,768]{1,0:T(8,128)} %fusion.24) | copy-start | bytes 7077892
  452.0 2.8 copy-start.2
  457.4 7.9 %slice-start = ((s8[4718592]{0:T(1024)(128)(4,1)}), s8[4194304]{0:T(1024)(128)(4,1)S(1)}, s32[]{:S(2)}) async-start(s8[4718592]{0:T(1024)(128)(4,1)} %bitcast.86), calls=%async_computation.7 | async-start | bytes 8388608
  459.9 5.4 slice-start.1
  461.9 3.4 copy-start.3
  473.4 96.4 %reduce-scatter.2.cloned.1.call-start = ((), (), s32[]{:S(2)}) async-start(), calls=%async_computation.6 | async-start | bytes 3932160 | tf_op jit(solution)/shard_map/reduce_scatter | solution.py:48
Sparse Core Ops, SparseCore 0:
  9.5 92.1 all-gather.2
  107.0 30.8 all-reduce.3
  147.4 63.6 all-gather.4
  473.5 30.3 all-reduce.5
  509.4 60.3 reduce-scatter.1
